TPU v7x, 32 devices: a whole 2x2x4 slice. The times are simulated.
32 devices in a mesh: slab: 2 (over y), date: 8 (over z, x), tile: 1, sub: 2 (over core).
Axes of the slice: x: 2, y: 2, z: 4, core: 2. Of those that a mesh axis runs over, the one named last changes fastest.
Arguments:
- slc: bfloat16 [2, 100, 128, 512], P(None, None, 'date', ('slab', 'tile', 'sub')), parts along dimension 3, may hold values from -300 to 300, as said below
- usable: int32 [100, 128, 512], P(None, 'date', ('slab', 'tile', 'sub')), parts along dimension 2, may hold values 0 or 1
Outputs:
- coherence: bfloat16 [2, 4, 8, 16, 128, 128], P(None, ('slab', 'tile', 'sub'), 'date'), parts along dimension 1
- linked: float32 [2, 128, 512], P(None, 'date', ('slab', 'tile', 'sub')), parts along dimension 2
There are 2 independent parts, one for each index of `slab`. A program takes and returns all parts, laid end to end along the dimension named above; each array names one. Nothing has to cross between parts.
Inputs may be any that keep to these rules, and one draw needn't show every extreme that they name: `slc`: complex samples of a partly coherent stack.
All inputs are finite; a program needn't handle non-finite values. No bound on the sum of `usable` on one device may be relied on, other than what follows from the above.
Results may differ from a plain program's by a relative error of at most 0.0016.
Values may be sent and summed in bfloat16 or wider, within the bound.
No kernel may reach another device: no remote copies, remote signals or barrier semaphores. Data moves between devices by JAX's collectives and lax.ppermute only.
A program may use at most 64 MiB of HBM per device.

v0:
```python
import jax
import jax.numpy as jnp
from jax import lax
from jax.sharding import PartitionSpec as P

ITERS = 4


def inverse_roots(block):
    samples = block.astype(jnp.float32)
    intensity = jnp.mean(samples[0] * samples[0] + samples[1] * samples[1], axis=0) + 1e-05
    return lax.rsqrt(intensity)


def pair_terms(left_block, right_block, left_root, right_root, looks_count):
    real_sum = jnp.einsum(
        "law,lbw->wab", left_block[0], right_block[0], preferred_element_type=jnp.float32
    )
    real_sum = real_sum + jnp.einsum(
        "law,lbw->wab", left_block[1], right_block[1], preferred_element_type=jnp.float32
    )
    imag_sum = jnp.einsum(
        "law,lbw->wab", left_block[1], right_block[0], preferred_element_type=jnp.float32
    )
    imag_sum = imag_sum - jnp.einsum(
        "law,lbw->wab", left_block[0], right_block[1], preferred_element_type=jnp.float32
    )
    factor = left_root.T[:, :, None] * right_root.T[:, None, :] * (1.0 / looks_count)
    return jnp.stack([real_sum * factor, imag_sum * factor])


def local_pairs(samples, looks_count):
    window_root = inverse_roots(samples)
    return pair_terms(samples, samples, window_root, window_root, looks_count).astype(jnp.bfloat16)


def complex_apply(matrix, vec_real, vec_imag):
    rr = jnp.einsum("wab,bw->aw", matrix[0], vec_real, precision=lax.Precision.HIGHEST)
    ii = jnp.einsum("wab,bw->aw", matrix[1], vec_imag, precision=lax.Precision.HIGHEST)
    ri = jnp.einsum("wab,bw->aw", matrix[0], vec_imag, precision=lax.Precision.HIGHEST)
    ir = jnp.einsum("wab,bw->aw", matrix[1], vec_real, precision=lax.Precision.HIGHEST)
    return (rr - ii, ri + ir)


def local(slc, usable):
    masked = slc * usable.astype(jnp.bfloat16)[None]
    looks_count = slc.shape[1]
    own_dates = slc.shape[2]
    windows = slc.shape[3]
    blocks_count = lax.axis_size("date")
    all_dates = own_dates * blocks_count
    per_device = windows // blocks_count
    split_view = masked.reshape(2, looks_count, own_dates, blocks_count, per_device)
    result = local_pairs(
        lax.all_to_all(split_view, "date", split_axis=3, concat_axis=2, tiled=True)[:, :, :, 0, :],
        looks_count,
    )
    matrix = result.astype(jnp.float32)
    vec_real = jnp.ones((all_dates, per_device), jnp.float32)
    vec_imag = jnp.zeros((all_dates, per_device), jnp.float32)
    for step in range(ITERS):
        new_real, new_imag = complex_apply(matrix, vec_real, vec_imag)
        scale = lax.rsqrt(jnp.mean(new_real * new_real + new_imag * new_imag, axis=0) + 1e-05)
        vec_real = new_real * scale[None]
        vec_imag = new_imag * scale[None]
    linked = lax.all_to_all(
        jnp.stack([vec_real, vec_imag]), "date", split_axis=1, concat_axis=2, tiled=True
    )
    return (result.reshape(2, 1, 1, per_device, all_dates, all_dates), linked)


def solution(mesh):
    return jax.shard_map(
        local,
        mesh=mesh,
        in_specs=(
            P(None, None, "date", ("slab", "tile", "sub")),
            P(None, "date", ("slab", "tile", "sub")),
        ),
        out_specs=(
            P(None, ("slab", "tile", "sub"), "date", None, None, None),
            P(None, "date", ("slab", "tile", "sub")),
        ),
        check_vma=False,
    )
```

profile of v0, /device:TPU:0, one launch (start us, length us, event | category | flops | bytes accessed | tf_op | source)
XLA Modules:
  0.0 69.2 jit_solution(11306917477091956717)
XLA Ops:
  0.6 1.9 %copy.78 = bf16[2,100,16,128]{1,3,2,0:T(8,128)(2,1)S(1)} copy(bf16[2,100,16,128]{3,2,1,0:T(8,128)(2,1)} %param.2) | data formatting | bytes 1638400 | tf_op args[0]
  3.5 32.8 %all_to_all.33 = bf16[2,100,16,8,16]{1,4,2,0,3:T(8,128)(2,1)S(1)} all-to-all(bf16[2,100,16,8,16]{1,4,2,0,3:T(8,128)(2,1)S(1)} %copy.79), channel_id=1, replica_groups=mesh['slab'=2,'date'=8,'tile'=1,'sub'=2] {'date'}, dimensions={3} | all-to-all | bytes 1638400 | tf_op jit(solution)/shard_map/all_to_all | solution.py:55
  39.3 0.9 %fusion.10 = f32[16,1,128]{2,1,0:T(1,128)S(1)} fusion(bf16[16,128,128]{2,1,0:T(8,128)(2,1)S(1)} %fusion.3), kind=kOutput, calls=%fused_computation.26 | convolution fusion | flops 3145728 | bytes 532480 | tf_op jit(solution)/shard_map/wab,bw->aw/dot_general | solution.py:39
  40.3 0.9 %fusion.12 = f32[16,1,128]{2,1,0:T(1,128)S(1)} fusion(bf16[16,128,128]{2,1,0:T(8,128)(2,1)S(1)} %fusion.3), kind=kOutput, calls=%fused_computation.28 | convolution fusion | flops 3145728 | bytes 532480 | tf_op jit(solution)/shard_map/wab,bw->aw/dot_general | solution.py:41
  42.1 0.9 %fusion.14 = f32[16,1,128]{2,1,0:T(1,128)S(1)} fusion(bf16[16,128,128]{2,1,0:T(8,128)(2,1)S(1)} %fusion.2), kind=kOutput, calls=%fused_computation.30 | convolution fusion | flops 3145728 | bytes 532480 | tf_op jit(solution)/shard_map/wab,bw->aw/dot_general | solution.py:38
  43.0 0.9 %fusion.8 = f32[16,1,128]{2,1,0:T(1,128)S(1)} fusion(bf16[16,128,128]{2,1,0:T(8,128)(2,1)S(1)} %fusion.2), kind=kOutput, calls=%fused_computation.24 | convolution fusion | flops 3145728 | bytes 532480 | tf_op jit(solution)/shard_map/wab,bw->aw/dot_general | solution.py:40
  44.1 0.9 %fusion.25 = f32[16,1,128]{2,1,0:T(1,128)S(1)} fusion(f32[128,16,1]{0,2,1:T(1,128)S(1)} %bitcast.144, bf16[16,128,128]{2,1,0:T(8,128)(2,1)S(1)} %fusion.2), kind=kOutput, calls=%fused_computation.52 | convolution fusion | flops 3145728 | bytes 540672 | tf_op jit(solution)/shard_map/wab,bw->aw/dot_general | solution.py:40
  45.1 0.9 %fusion.24 = f32[16,1,128]{2,1,0:T(1,128)S(1)} fusion(f32[128,16,1]{0,2,1:T(1,128)S(1)} %bitcast.145, bf16[16,128,128]{2,1,0:T(8,128)(2,1)S(1)} %fusion.3), kind=kOutput, calls=%fused_computation.51 | convolution fusion | flops 3145728 | bytes 540672 | tf_op jit(solution)/shard_map/wab,bw->aw/dot_general | solution.py:39
  46.0 0.9 %fusion.26 = f32[16,1,128]{2,1,0:T(1,128)S(1)} fusion(f32[128,16,1]{0,2,1:T(1,128)S(1)} %bitcast.138, bf16[16,128,128]{2,1,0:T(8,128)(2,1)S(1)} %fusion.3), kind=kOutput, calls=%fused_computation.53 | convolution fusion | flops 3145728 | bytes 540672 | tf_op jit(solution)/shard_map/wab,bw->aw/dot_general | solution.py:41
  46.9 0.9 %fusion.23 = f32[16,1,128]{2,1,0:T(1,128)S(1)} fusion(f32[128,16,1]{0,2,1:T(1,128)S(1)} %bitcast.139, bf16[16,128,128]{2,1,0:T(8,128)(2,1)S(1)} %fusion.2), kind=kOutput, calls=%fused_computation.50 | convolution fusion | flops 3145728 | bytes 540672 | tf_op jit(solution)/shard_map/wab,bw->aw/dot_general | solution.py:38
  48.0 0.9 %fusion.29 = f32[16,1,128]{2,1,0:T(1,128)S(1)} fusion(f32[128,16,1]{0,2,1:T(1,128)S(1)} %bitcast.146, bf16[16,128,128]{2,1,0:T(8,128)(2,1)S(1)} %fusion.2), kind=kOutput, calls=%fused_computation.56 | convolution fusion | flops 3145728 | bytes 540672 | tf_op jit(solution)/shard_map/wab,bw->aw/dot_general | solution.py:40
  49.0 0.9 %fusion.28 = f32[16,1,128]{2,1,0:T(1,128)S(1)} fusion(f32[128,16,1]{0,2,1:T(1,128)S(1)} %bitcast.147, bf16[16,128,128]{2,1,0:T(8,128)(2,1)S(1)} %fusion.3), kind=kOutput, calls=%fused_computation.55 | convolution fusion | flops 3145728 | bytes 540672 | tf_op jit(solution)/shard_map/wab,bw->aw/dot_general | solution.py:39
  49.9 0.9 %fusion.30 = f32[16,1,128]{2,1,0:T(1,128)S(1)} fusion(f32[128,16,1]{0,2,1:T(1,128)S(1)} %bitcast.140, bf16[16,128,128]{2,1,0:T(8,128)(2,1)S(1)} %fusion.3), kind=kOutput, calls=%fused_computation.57 | convolution fusion | flops 3145728 | bytes 540672 | tf_op jit(solution)/shard_map/wab,bw->aw/dot_general | solution.py:41
  50.8 0.9 %fusion.27 = f32[16,1,128]{2,1,0:T(1,128)S(1)} fusion(f32[128,16,1]{0,2,1:T(1,128)S(1)} %bitcast.141, bf16[16,128,128]{2,1,0:T(8,128)(2,1)S(1)} %fusion.2), kind=kOutput, calls=%fused_computation.54 | convolution fusion | flops 3145728 | bytes 540672 | tf_op jit(solution)/shard_map/wab,bw->aw/dot_general | solution.py:38
  52.0 0.9 %fusion.33 = f32[16,1,128]{2,1,0:T(1,128)S(1)} fusion(f32[128,16,1]{0,2,1:T(1,128)S(1)} %bitcast.148, bf16[16,128,128]{2,1,0:T(8,128)(2,1)S(1)} %fusion.2), kind=kOutput, calls=%fused_computation.60 | convolution fusion | flops 3145728 | bytes 540672 | tf_op jit(solution)/shard_map/wab,bw->aw/dot_general | solution.py:40
  52.9 0.9 %fusion.32 = f32[16,1,128]{2,1,0:T(1,128)S(1)} fusion(f32[128,16,1]{0,2,1:T(1,128)S(1)} %bitcast.149, bf16[16,128,128]{2,1,0:T(8,128)(2,1)S(1)} %fusion.3), kind=kOutput, calls=%fused_computation.59 | convolution fusion | flops 3145728 | bytes 540672 | tf_op jit(solution)/shard_map/wab,bw->aw/dot_general | solution.py:39
  53.8 0.9 %fusion.34 = f32[16,1,128]{2,1,0:T(1,128)S(1)} fusion(f32[128,16,1]{0,2,1:T(1,128)S(1)} %bitcast.142, bf16[16,128,128]{2,1,0:T(8,128)(2,1)S(1)} %fusion.3), kind=kOutput, calls=%fused_computation.61 | convolution fusion | flops 3145728 | bytes 540672 | tf_op jit(solution)/shard_map/wab,bw->aw/dot_general | solution.py:41
  54.7 0.9 %fusion.31 = f32[16,1,128]{2,1,0:T(1,128)S(1)} fusion(f32[128,16,1]{0,2,1:T(1,128)S(1)} %bitcast.143, bf16[16,128,128]{2,1,0:T(8,128)(2,1)S(1)} %fusion.2), kind=kOutput, calls=%fused_computation.58 | convolution fusion | flops 3145728 | bytes 540672 | tf_op jit(solution)/shard_map/wab,bw->aw/dot_general | solution.py:38
  56.0 0.8 %reshape.118 = f32[8,1,512]{2,1,0:T(1,128)} reshape(f32[128,2,16]{2,1,0:T(2,128)S(1)} %bitcast.133) | data formatting | bytes 32768
  56.8 3.6 %all-to-all-start.1 = ((f32[8,1,512]{2,1,0:T(1,128)}), f32[8,1,512]{2,1,0:T(1,128)S(1)}, u32[]{:S(2)}, u32[]{:S(2)}) async-start(f32[8,1,512]{2,1,0:T(1,128)} %reshape.118), calls=%async_computation.1 | async-start | bytes 32768 | tf_op jit(solution)/shard_map/all_to_all | solution.py:66
  60.4 1.1 %pad_maximum_fusion = bf16[2,1,1,16,128,128]{5,4,3,2,1,0:T(8,128)(2,1)} fusion(bf16[1,1,1,16,128,128]{5,4,3,2,1,0:T(8,128)(2,1)S(1)} %bitcast.127, bf16[1,1,1,16,128,128]{5,4,3,2,1,0:T(8,128)(2,1)S(1)} %bitcast.128), kind=kLoop, calls=%fused_computation.10 | loop fusion | flops 524288 | bytes 2097152 | tf_op jit(solution)/shard_map/stack | solution.py:29
  61.5 5.5 %all-to-all-done.1 = f32[8,1,512]{2,1,0:T(1,128)S(1)} async-done(((f32[8,1,512]{2,1,0:T(1,128)}), f32[8,1,512]{2,1,0:T(1,128)S(1)}, u32[]{:S(2)}, u32[]{:S(2)}) %all-to-all-start.1) | async-done | bytes 16416 | tf_op jit(solution)/shard_map/all_to_all | solution.py:66
  67.5 0.7 reduce.7
  68.5 0.7 %all_to_all.30 = f32[2,16,128]{2,1,0:T(8,128)} reshape(f32[2,16,8,16]{3,2,1,0:T(8,128)S(1)} %bitcast.135) | data formatting | bytes 32768 | tf_op jit(solution)/shard_map/all_to_all | solution.py:66
  (35 shorter events, 6.5 us)
Async XLA Ops:
  0.6 2.0 %copy-start = (s32[100,16,128]{2,1,0:T(8,128)S(1)}, s32[100,16,128]{2,1,0:T(8,128)}, u32[]{:S(2)}) copy-start(s32[100,16,128]{2,1,0:T(8,128)} %param.3) | copy-start | bytes 2457604
  56.8 10.2 %all-to-all-start.1 = ((f32[8,1,512]{2,1,0:T(1,128)}), f32[8,1,512]{2,1,0:T(1,128)S(1)}, u32[]{:S(2)}, u32[]{:S(2)}) async-start(f32[8,1,512]{2,1,0:T(1,128)} %reshape.118), calls=%async_computation.1 | async-start | bytes 32768 | tf_op jit(solution)/shard_map/all_to_all | solution.py:66
where the time goes:
time: 69.4 us; the launch traced here: 69.2 us
  blocking collectives  32.8 us (47%)
  matrix products  16.5 us (24%)
  local copies, waits for them, and re-layouts  6.56 us (9%)
  waiting for transfers between devices  5.51 us (8%)
  starting transfers between devices  3.59 us (5%)
  other arithmetic  3.35 us (5%)
  between operations  0.82 us (1%)
    all_to_all x1, blocking collectives, local(): lax.all_to_all(split_view, 'date', split_axis=3, concat_axis=2, tiled=True)  32.8 us
    all_to_all x1, waiting for transfers between devices, local(): lax.all_to_all(jnp.stack([vec_real, vec_imag]), 'date', split_axis=1, con...  5.51 us
    dot_general x4, matrix products, complex_apply(): jnp.einsum('wab,bw->aw', matrix[1], vec_real, precision=lax.Precision.HIG...  3.7 us
    dot_general x4, matrix products, complex_apply(): jnp.einsum('wab,bw->aw', matrix[0], vec_imag, precision=lax.Precision.HIG...  3.68 us
    dot_general x4, matrix products, complex_apply(): jnp.einsum('wab,bw->aw', matrix[0], vec_real, precision=lax.Precision.HIG...  3.68 us
    dot_general x4, matrix products, complex_apply(): jnp.einsum('wab,bw->aw', matrix[1], vec_imag, precision=lax.Precision.HIG...  3.68 us
    all_to_all x1, starting transfers between devices, local(): lax.all_to_all(jnp.stack([vec_real, vec_imag]), 'date', split_axis=1, con...  3.59 us
    unnamed x5, local copies, waits for them, and re-layouts  2.95 us
  transfers between devices with their start and end apart: 1, of which 1 were waited for; matrix products, arithmetic and copies ran while one was open for 2% of the time, Pallas kernels for 0%

commit v1 on v0

--- a/solution.py
+++ b/solution.py
@@ -63,9 +63,16 @@
         scale = lax.rsqrt(jnp.mean(new_real * new_real + new_imag * new_imag, axis=0) + 1e-05)
         vec_real = new_real * scale[None]
         vec_imag = new_imag * scale[None]
-    linked = lax.all_to_all(
-        jnp.stack([vec_real, vec_imag]), "date", split_axis=1, concat_axis=2, tiled=True
-    )
+    array = jnp.stack([vec_real, vec_imag])
+    ways, here = (lax.axis_size("date"), lax.axis_index("date"))
+    width = array.shape[1] // ways
+    turned = jnp.roll(array, -here * width, axis=1)
+    got = [lax.slice_in_dim(turned, 0, width, axis=1)]
+    for far in range(1, ways):
+        sent = lax.slice_in_dim(turned, far * width, (far + 1) * width, axis=1)
+        got.append(lax.ppermute(sent, "date", [(d, (d + far) % ways) for d in range(ways)]))
+    line = jnp.concatenate(got[::-1], axis=2)
+    linked = jnp.roll(line, (here + 1) * got[0].shape[2], axis=2)
     return (result.reshape(2, 1, 1, per_device, all_dates, all_dates), linked)
 
 

time: 69.4 us -> 72.1 us (1.039)
  blocking collectives: 32.8 us -> 0 us
  waiting for transfers between devices: 5.51 us -> 29.2 us
  starting transfers between devices: 3.59 us -> 16.1 us
    all_to_all x1 -> x0, blocking collectives: 32.8 us -> none  [local(): lax.all_to_all(split_view, 'date', split_axis=3, concat_axis=2, tiled=True)]
    all_to_all x1, waiting for transfers between devices: 5.51 us -> 25.8 us  [local(): lax.all_to_all(split_view, 'date', split_axis=3, concat_axis=2, tiled=True)]
    ppermute x0 -> x7, starting transfers between devices: none -> 8.78 us  [local(): lax.ppermute(sent, 'date', [(d, (d + far) % ways) for d in range(ways)])]
    all_to_all x1, starting transfers between devices: 3.59 us -> 7.28 us  [local(): lax.all_to_all(split_view, 'date', split_axis=3, concat_axis=2, tiled=True)]
    ppermute x0 -> x7, waiting for transfers between devices: none -> 3.48 us  [local(): lax.ppermute(sent, 'date', [(d, (d + far) % ways) for d in range(ways)])]
    all_to_all x3 -> x0, local copies, waits for them, and re-layouts: 1.3 us -> none  [local(): lax.all_to_all(jnp.stack([vec_real, vec_imag]), 'date', split_axis=1, con...]
    unnamed x5 -> x3, local copies, waits for them, and re-layouts: 2.95 us -> 1.94 us
    reshape x1, local copies, waits for them, and re-layouts: 0.27 us -> 1.24 us  [local(): masked.reshape(2, looks_count, own_dates, blocks_count, per_device)]
  transfers between devices with their start and end apart: 1 -> 8, of which waited for: 1 -> 4; matrix products, arithmetic and copies ran while one was open for 2% -> 2% of each run, Pallas kernels for 0% -> 0%
where the time goes in v1:
time: 72.1 us; the launch traced here: 72 us
  waiting for transfers between devices  29.2 us (40%)
  matrix products  16.5 us (23%)
  starting transfers between devices  16.1 us (22%)
  local copies, waits for them, and re-layouts  6.56 us (9%)
  other arithmetic  2.74 us (4%)
  between operations  0.81 us (1%)
    all_to_all x1, waiting for transfers between devices, local(): lax.all_to_all(split_view, 'date', split_axis=3, concat_axis=2, tiled=True)  25.8 us
    ppermute x7, starting transfers between devices, local(): lax.ppermute(sent, 'date', [(d, (d + far) % ways) for d in range(ways)])  8.78 us
    all_to_all x1, starting transfers between devices, local(): lax.all_to_all(split_view, 'date', split_axis=3, concat_axis=2, tiled=True)  7.28 us
    dot_general x4, matrix products, complex_apply(): jnp.einsum('wab,bw->aw', matrix[0], vec_imag, precision=lax.Precision.HIG...  3.7 us
    dot_general x4, matrix products, complex_apply(): jnp.einsum('wab,bw->aw', matrix[1], vec_real, precision=lax.Precision.HIG...  3.7 us
    dot_general x4, matrix products, complex_apply(): jnp.einsum('wab,bw->aw', matrix[1], vec_imag, precision=lax.Precision.HIG...  3.68 us
    dot_general x4, matrix products, complex_apply(): jnp.einsum('wab,bw->aw', matrix[0], vec_real, precision=lax.Precision.HIG...  3.67 us
    ppermute x7, waiting for transfers between devices, local(): lax.ppermute(sent, 'date', [(d, (d + far) % ways) for d in range(ways)])  3.48 us
  transfers between devices with their start and end apart: 8, of which 4 were waited for; matrix products, arithmetic and copies ran while one was open for 2% of the time, Pallas kernels for 0%

profile of v1, /device:TPU:0, one launch (start us, length us, event | category | flops | bytes accessed | tf_op | source)
XLA Modules:
  0.0 72.0 jit_solution(125433265288515688)
XLA Ops:
  0.6 1.9 %copy.74 = bf16[2,100,16,128]{1,3,2,0:T(8,128)(2,1)S(1)} copy(bf16[2,100,16,128]{3,2,1,0:T(8,128)(2,1)} %param.2) | data formatting | bytes 1638400 | tf_op args[0]
  3.2 1.2 %copy.75 = bf16[2,100,16,8,16]{1,4,2,0,3:T(8,128)(2,1)} copy(bf16[2,100,16,8,16]{1,4,3,2,0:T(8,128)(2,1)S(1)} %bitcast.121) | data formatting | bytes 1638400 | tf_op jit(solution)/shard_map/reshape | solution.py:53
  4.5 7.3 %all-to-all-start = ((bf16[2,100,16,8,16]{1,4,2,0,3:T(8,128)(2,1)}), bf16[2,100,16,8,16]{1,4,2,0,3:T(8,128)(2,1)S(1)}, u32[]{:S(2)}, u32[]{:S(2)}) async-start(bf16[2,100,16,8,16]{1,4,2,0,3:T(8,128)(2,1)} %copy.75), calls=%async_computation | async-start | bytes 2097152 | tf_op jit(solution)/shard_map/all_to_all | solution.py:55
  11.7 25.8 %all-to-all-done = bf16[2,100,16,8,16]{1,4,2,0,3:T(8,128)(2,1)S(1)} async-done(((bf16[2,100,16,8,16]{1,4,2,0,3:T(8,128)(2,1)}), bf16[2,100,16,8,16]{1,4,2,0,3:T(8,128)(2,1)S(1)}, u32[]{:S(2)}, u32[]{:S(2)}) %all-to-all-start) | async-done | bytes 819232 | tf_op jit(solution)/shard_map/all_to_all | solution.py:55
  41.4 0.9 %fusion.15 = f32[16,1,128]{2,1,0:T(1,128)S(1)} fusion(bf16[16,128,128]{2,1,0:T(8,128)(2,1)S(1)} %fusion.3), kind=kOutput, calls=%fused_computation.33 | convolution fusion | flops 3145728 | bytes 532480 | tf_op jit(solution)/shard_map/wab,bw->aw/dot_general | solution.py:41
  44.2 0.9 %fusion.11 = f32[16,1,128]{2,1,0:T(1,128)S(1)} fusion(bf16[16,128,128]{2,1,0:T(8,128)(2,1)S(1)} %fusion.2), kind=kOutput, calls=%fused_computation.29 | convolution fusion | flops 3145728 | bytes 532480 | tf_op jit(solution)/shard_map/wab,bw->aw/dot_general | solution.py:40
  45.3 0.9 %fusion.27 = f32[16,1,128]{2,1,0:T(1,128)S(1)} fusion(f32[128,16,1]{0,2,1:T(1,128)S(1)} %bitcast.132, bf16[16,128,128]{2,1,0:T(8,128)(2,1)S(1)} %fusion.2), kind=kOutput, calls=%fused_computation.57 | convolution fusion | flops 3145728 | bytes 540672 | tf_op jit(solution)/shard_map/wab,bw->aw/dot_general | solution.py:38
  46.2 0.9 %fusion.30 = f32[16,1,128]{2,1,0:T(1,128)S(1)} fusion(f32[128,16,1]{0,2,1:T(1,128)S(1)} %bitcast.133, bf16[16,128,128]{2,1,0:T(8,128)(2,1)S(1)} %fusion.3), kind=kOutput, calls=%fused_computation.60 | convolution fusion | flops 3145728 | bytes 540672 | tf_op jit(solution)/shard_map/wab,bw->aw/dot_general | solution.py:41
  47.2 0.9 %fusion.28 = f32[16,1,128]{2,1,0:T(1,128)S(1)} fusion(f32[128,16,1]{0,2,1:T(1,128)S(1)} %bitcast.126, bf16[16,128,128]{2,1,0:T(8,128)(2,1)S(1)} %fusion.3), kind=kOutput, calls=%fused_computation.58 | convolution fusion | flops 3145728 | bytes 540672 | tf_op jit(solution)/shard_map/wab,bw->aw/dot_general | solution.py:39
  48.1 0.9 %fusion.29 = f32[16,1,128]{2,1,0:T(1,128)S(1)} fusion(f32[128,16,1]{0,2,1:T(1,128)S(1)} %bitcast.127, bf16[16,128,128]{2,1,0:T(8,128)(2,1)S(1)} %fusion.2), kind=kOutput, calls=%fused_computation.59 | convolution fusion | flops 3145728 | bytes 540672 | tf_op jit(solution)/shard_map/wab,bw->aw/dot_general | solution.py:40
  49.2 0.9 %fusion.31 = f32[16,1,128]{2,1,0:T(1,128)S(1)} fusion(f32[128,16,1]{0,2,1:T(1,128)S(1)} %bitcast.134, bf16[16,128,128]{2,1,0:T(8,128)(2,1)S(1)} %fusion.2), kind=kOutput, calls=%fused_computation.61 | convolution fusion | flops 3145728 | bytes 540672 | tf_op jit(solution)/shard_map/wab,bw->aw/dot_general | solution.py:38
  50.1 0.9 %fusion.34 = f32[16,1,128]{2,1,0:T(1,128)S(1)} fusion(f32[128,16,1]{0,2,1:T(1,128)S(1)} %bitcast.135, bf16[16,128,128]{2,1,0:T(8,128)(2,1)S(1)} %fusion.3), kind=kOutput, calls=%fused_computation.64 | convolution fusion | flops 3145728 | bytes 540672 | tf_op jit(solution)/shard_map/wab,bw->aw/dot_general | solution.py:41
  51.1 0.9 %fusion.32 = f32[16,1,128]{2,1,0:T(1,128)S(1)} fusion(f32[128,16,1]{0,2,1:T(1,128)S(1)} %bitcast.128, bf16[16,128,128]{2,1,0:T(8,128)(2,1)S(1)} %fusion.3), kind=kOutput, calls=%fused_computation.62 | convolution fusion | flops 3145728 | bytes 540672 | tf_op jit(solution)/shard_map/wab,bw->aw/dot_general | solution.py:39
  52.0 0.9 %fusion.33 = f32[16,1,128]{2,1,0:T(1,128)S(1)} fusion(f32[128,16,1]{0,2,1:T(1,128)S(1)} %bitcast.129, bf16[16,128,128]{2,1,0:T(8,128)(2,1)S(1)} %fusion.2), kind=kOutput, calls=%fused_computation.63 | convolution fusion | flops 3145728 | bytes 540672 | tf_op jit(solution)/shard_map/wab,bw->aw/dot_general | solution.py:40
  54.1 0.9 %fusion.38 = f32[16,1,128]{2,1,0:T(1,128)S(1)} fusion(f32[128,16,1]{0,2,1:T(1,128)S(1)} %bitcast.137, bf16[16,128,128]{2,1,0:T(8,128)(2,1)S(1)} %fusion.3), kind=kOutput, calls=%fused_computation.68 | convolution fusion | flops 3145728 | bytes 540672 | tf_op jit(solution)/shard_map/wab,bw->aw/dot_general | solution.py:41
  55.0 0.9 %fusion.36 = f32[16,1,128]{2,1,0:T(1,128)S(1)} fusion(f32[128,16,1]{0,2,1:T(1,128)S(1)} %bitcast.130, bf16[16,128,128]{2,1,0:T(8,128)(2,1)S(1)} %fusion.3), kind=kOutput, calls=%fused_computation.66 | convolution fusion | flops 3145728 | bytes 540672 | tf_op jit(solution)/shard_map/wab,bw->aw/dot_general | solution.py:39
  55.9 0.9 %fusion.37 = f32[16,1,128]{2,1,0:T(1,128)S(1)} fusion(f32[128,16,1]{0,2,1:T(1,128)S(1)} %bitcast.131, bf16[16,128,128]{2,1,0:T(8,128)(2,1)S(1)} %fusion.2), kind=kOutput, calls=%fused_computation.67 | convolution fusion | flops 3145728 | bytes 540672 | tf_op jit(solution)/shard_map/wab,bw->aw/dot_general | solution.py:40
  57.2 2.4 %collective-permute-start = (f32[2,16,16]{1,2,0:T(8,128)S(1)}, f32[2,16,16]{1,2,0:T(8,128)S(1)}, u32[]{:S(2)}, u32[]{:S(2)}) collective-permute-start(f32[2,16,16]{1,2,0:T(8,128)S(1)} %get-tuple-element.27), channel_id=1, source_target_pairs={{0,14},{2,0},{4,2},{6,4},{8,6},{10,8},{12,10},{14,12},{1,15},{3,1}... | collective-permute-start | bytes 6152 | tf_op jit(solution)/shard_map/ppermute | solution.py:73
  59.8 3.0 %collective-permute-start.3 = (f32[2,16,16]{1,2,0:T(8,128)S(1)}, f32[2,16,16]{1,2,0:T(8,128)S(1)}, u32[]{:S(2)}, u32[]{:S(2)}) collective-permute-start(f32[2,16,16]{1,2,0:T(8,128)S(1)} %get-tuple-element.24), channel_id=1, source_target_pairs={{0,8},{2,10},{4,12},{6,14},{8,0},{10,2},{12,4},{14,6},{1,9},{3,11}... | collective-permute-start | bytes 6152 | tf_op jit(solution)/shard_map/ppermute | solution.py:73
  62.9 1.7 %collective-permute-start.4 = (f32[2,16,16]{1,2,0:T(8,128)S(1)}, f32[2,16,16]{1,2,0:T(8,128)S(1)}, u32[]{:S(2)}, u32[]{:S(2)}) collective-permute-start(f32[2,16,16]{1,2,0:T(8,128)S(1)} %get-tuple-element.23), channel_id=1, source_target_pairs={{0,6},{2,8},{4,10},{6,12},{8,14},{10,0},{12,2},{14,4},{1,7},{3,9},... | collective-permute-start | bytes 6152 | tf_op jit(solution)/shard_map/ppermute | solution.py:73
  64.6 1.5 %collective-permute-start.6 = (f32[2,16,16]{1,2,0:T(8,128)S(1)}, f32[2,16,16]{1,2,0:T(8,128)S(1)}, u32[]{:S(2)}, u32[]{:S(2)}) collective-permute-start(f32[2,16,16]{1,2,0:T(8,128)S(1)} %get-tuple-element.21), channel_id=1, source_target_pairs={{0,2},{2,4},{4,6},{6,8},{8,10},{10,12},{12,14},{14,0},{1,3},{3,5},... | collective-permute-start | bytes 6152 | tf_op jit(solution)/shard_map/ppermute | solution.py:73
  66.0 1.1 %pad_maximum_fusion = bf16[2,1,1,16,128,128]{5,4,3,2,1,0:T(8,128)(2,1)} fusion(bf16[1,1,1,16,128,128]{5,4,3,2,1,0:T(8,128)(2,1)S(1)} %bitcast.118, bf16[1,1,1,16,128,128]{5,4,3,2,1,0:T(8,128)(2,1)S(1)} %bitcast.119), kind=kLoop, calls=%fused_computation.10 | loop fusion | flops 524288 | bytes 2097152 | tf_op jit(solution)/shard_map/stack | solution.py:29
  67.5 0.9 %collective-permute-done.4 = f32[2,16,16]{1,2,0:T(8,128)S(1)} collective-permute-done((f32[2,16,16]{1,2,0:T(8,128)S(1)}, f32[2,16,16]{1,2,0:T(8,128)S(1)}, u32[]{:S(2)}, u32[]{:S(2)}) %collective-permute-start.4) | collective-permute-done | bytes 2080 | tf_op jit(solution)/shard_map/ppermute | solution.py:73
  68.5 1.6 %collective-permute-done.5 = f32[2,16,16]{1,2,0:T(8,128)S(1)} collective-permute-done((f32[2,16,16]{1,2,0:T(8,128)S(1)}, f32[2,16,16]{1,2,0:T(8,128)S(1)}, u32[]{:S(2)}, u32[]{:S(2)}) %collective-permute-start.5) | collective-permute-done | bytes 2080 | tf_op jit(solution)/shard_map/ppermute | solution.py:73
  (52 shorter events, 10.7 us)
Async XLA Ops:
  0.6 2.0 %copy-start = (s32[100,16,128]{2,1,0:T(8,128)S(1)}, s32[100,16,128]{2,1,0:T(8,128)}, u32[]{:S(2)}) copy-start(s32[100,16,128]{2,1,0:T(8,128)} %param.3) | copy-start | bytes 2457604
  4.5 33.0 %all-to-all-start = ((bf16[2,100,16,8,16]{1,4,2,0,3:T(8,128)(2,1)}), bf16[2,100,16,8,16]{1,4,2,0,3:T(8,128)(2,1)S(1)}, u32[]{:S(2)}, u32[]{:S(2)}) async-start(bf16[2,100,16,8,16]{1,4,2,0,3:T(8,128)(2,1)} %copy.75), calls=%async_computation | async-start | bytes 2097152 | tf_op jit(solution)/shard_map/all_to_all | solution.py:55
  57.2 7.3 %collective-permute-start = (f32[2,16,16]{1,2,0:T(8,128)S(1)}, f32[2,16,16]{1,2,0:T(8,128)S(1)}, u32[]{:S(2)}, u32[]{:S(2)}) collective-permute-start(f32[2,16,16]{1,2,0:T(8,128)S(1)} %get-tuple-element.27), channel_id=1, source_target_pairs={{0,14},{2,0},{4,2},{6,4},{8,6},{10,8},{12,10},{14,12},{1,15},{3,1}... | collective-permute-start | bytes 6152 | tf_op jit(solution)/shard_map/ppermute | solution.py:73
  59.6 5.0 %collective-permute-start.1 = (f32[2,16,16]{1,2,0:T(8,128)S(1)}, f32[2,16,16]{1,2,0:T(8,128)S(1)}, u32[]{:S(2)}, u32[]{:S(2)}) collective-permute-start(f32[2,16,16]{1,2,0:T(8,128)S(1)} %get-tuple-element.26), channel_id=1, source_target_pairs={{0,12},{2,14},{4,0},{6,2},{8,4},{10,6},{12,8},{14,10},{1,13},{3,15... | collective-permute-start | bytes 6152 | tf_op jit(solution)/shard_map/ppermute | solution.py:73
  59.6 7.7 %collective-permute-start.2 = (f32[2,16,16]{1,2,0:T(8,128)S(1)}, f32[2,16,16]{1,2,0:T(8,128)S(1)}, u32[]{:S(2)}, u32[]{:S(2)}) collective-permute-start(f32[2,16,16]{1,2,0:T(8,128)S(1)} %get-tuple-element.25), channel_id=1, source_target_pairs={{0,10},{2,12},{4,14},{6,0},{8,2},{10,4},{12,6},{14,8},{1,11},{3,13... | collective-permute-start | bytes 6152 | tf_op jit(solution)/shard_map/ppermute | solution.py:73
  59.8 7.6 %collective-permute-start.3 = (f32[2,16,16]{1,2,0:T(8,128)S(1)}, f32[2,16,16]{1,2,0:T(8,128)S(1)}, u32[]{:S(2)}, u32[]{:S(2)}) collective-permute-start(f32[2,16,16]{1,2,0:T(8,128)S(1)} %get-tuple-element.24), channel_id=1, source_target_pairs={{0,8},{2,10},{4,12},{6,14},{8,0},{10,2},{12,4},{14,6},{1,9},{3,11}... | collective-permute-start | bytes 6152 | tf_op jit(solution)/shard_map/ppermute | solution.py:73
  62.9 5.5 %collective-permute-start.4 = (f32[2,16,16]{1,2,0:T(8,128)S(1)}, f32[2,16,16]{1,2,0:T(8,128)S(1)}, u32[]{:S(2)}, u32[]{:S(2)}) collective-permute-start(f32[2,16,16]{1,2,0:T(8,128)S(1)} %get-tuple-element.23), channel_id=1, source_target_pairs={{0,6},{2,8},{4,10},{6,12},{8,14},{10,0},{12,2},{14,4},{1,7},{3,9},... | collective-permute-start | bytes 6152 | tf_op jit(solution)/shard_map/ppermute | solution.py:73
  64.6 5.5 %collective-permute-start.5 = (f32[2,16,16]{1,2,0:T(8,128)S(1)}, f32[2,16,16]{1,2,0:T(8,128)S(1)}, u32[]{:S(2)}, u32[]{:S(2)}) collective-permute-start(f32[2,16,16]{1,2,0:T(8,128)S(1)} %get-tuple-element.22), channel_id=1, source_target_pairs={{0,4},{2,6},{4,8},{6,10},{8,12},{10,14},{12,0},{14,2},{1,5},{3,7},... | collective-permute-start | bytes 6152 | tf_op jit(solution)/shard_map/ppermute | solution.py:73
  64.6 6.5 %collective-permute-start.6 = (f32[2,16,16]{1,2,0:T(8,128)S(1)}, f32[2,16,16]{1,2,0:T(8,128)S(1)}, u32[]{:S(2)}, u32[]{:S(2)}) collective-permute-start(f32[2,16,16]{1,2,0:T(8,128)S(1)} %get-tuple-element.21), channel_id=1, source_target_pairs={{0,2},{2,4},{4,6},{6,8},{8,10},{10,12},{12,14},{14,0},{1,3},{3,5},... | collective-permute-start | bytes 6152 | tf_op jit(solution)/shard_map/ppermute | solution.py:73
